TPU v7x, 512 devices: a whole 4x8x8 slice. The times are simulated.
512 devices in a mesh: seq: 128 (over x, z, y_lo), head: 4 (over y_hi, core).
Axes of the slice: x: 4, y: 8 (y_hi: 2, y_lo: 4; y = y_hi * 4 + y_lo), z: 8, core: 2. Of those that a mesh axis runs over, the one named last changes fastest.
Arguments:
- features: bfloat16 [32768, 1024], P('seq', 'head'), may hold values from -6 to 6
- w_query: bfloat16 [1024, 512], P(None, 'head'), may hold values from -0.1875 to 0.1875
- w_key: bfloat16 [1024, 512], P(None, 'head'), may hold values from -0.1875 to 0.1875
- w_value: bfloat16 [1024, 1024], P(None, 'head'), may hold values from -0.1875 to 0.1875
- w_gate: bfloat16 [1024, 1024], P(None, 'head'), may hold values from -0.1875 to 0.1875
- w_out: bfloat16 [1024, 1024], replicated, may hold values from -0.1875 to 0.1875
- forget: bfloat16 [2, 32768, 512], P(None, 'seq', 'head'), may hold values from -2.5 to 0, as said below
Outputs:
- encoded: bfloat16 [32768, 1024], P('seq', 'head')
Inputs may be any that keep to these rules, and one draw needn't show every extreme that they name: `forget`: every entry is below zero.
All inputs are finite; a program needn't handle non-finite values.
Results may differ from a plain program's by a relative error of at most 0.013.
Values may be sent and summed in bfloat16 or wider, within the bound.
A program may use at most 64 MiB of HBM per device.

v0:
```python
import jax
import jax.numpy as jnp
from jax import lax
from jax.sharding import Mesh
from jax.sharding import PartitionSpec as P

HEAD_K = 64
HEAD_V = 128
GROUP = 64
SEQ = ("seq_0", "seq_1", "seq_2")


def from_everyone(shard, axis):
    copies = jnp.broadcast_to(shard, (lax.axis_size(axis), *shard.shape))
    return lax.all_to_all(copies, axis, split_axis=0, concat_axis=0, tiled=True)


def in_order(tiles, dim):
    dims = list(tiles.shape[1:])
    dims[dim] *= tiles.shape[0]
    return jnp.moveaxis(tiles, 0, dim).reshape(dims)


def collect(shard, axis, dim):
    tiles = from_everyone(shard, axis)
    return in_order(tiles, dim)


def nothing_yet(shard, identity):
    return jax.tree.map(
        lambda a, e: jnp.broadcast_to(jnp.asarray(e, a.dtype), a.shape), shard, identity
    )


def gathered_once(shard, axis):
    leaves = jax.tree.leaves(shard)
    order = sorted(range(len(leaves)), key=lambda k: -leaves[k].size)
    width = (1, *leaves[order[0]].shape)[-1]
    lines = [
        jnp.pad(leaves[k].reshape(-1), (0, -leaves[k].size % width)).reshape(-1, width)
        for k in order
    ]
    both, at, found = (lax.all_gather(jnp.concatenate(lines), axis), 0, {})
    for k, line in zip(order, lines):
        slab = both[:, at : at + len(line)].reshape(len(both), -1)
        found[k] = slab[:, : leaves[k].size].reshape(-1, *leaves[k].shape)
        at += len(line)
    numbers = iter(range(len(leaves)))
    return jax.tree.map(lambda _: found[next(numbers)], shard)


def prefix_by_axis(shard, axes, combine, identity):
    before = start = nothing_yet(shard, identity)
    so_far = shard
    for axis in reversed(axes):
        peers, place = (lax.axis_size(axis), lax.axis_index(axis))
        pieces = gathered_once(so_far, axis)
        inside, so_far = (start, start)
        for k in range(peers):
            passed = k < place
            so_far = combine(so_far, jax.tree.map(lambda part: part[k], pieces))
            inside = jax.tree.map(lambda new, old: jnp.where(passed, new, old), so_far, inside)
        before = combine(inside, before)
    return before


def carried_in(shard, axes, combine, identity):
    before = start = nothing_yet(shard, identity)
    so_far = shard
    for axis in reversed(axes):
        peers, place = (lax.axis_size(axis), lax.axis_index(axis))
        pieces = gathered_once(
            jax.tree.map(
                lambda part, kind: part.astype(kind), so_far, (jnp.bfloat16, jnp.bfloat16)
            ),
            axis,
        )
        inside, so_far = (start, start)
        for k in reversed(range(peers)):
            passed = k > place
            so_far = combine(
                so_far, jax.tree.map(lambda part, own: part[k].astype(own.dtype), pieces, shard)
            )
            inside = jax.tree.map(lambda new, old: jnp.where(passed, new, old), so_far, inside)
        before = combine(inside, before)
    return before


def to_blocks(tensor):
    block_count = tensor.shape[0] // GROUP
    return tensor.reshape((block_count, GROUP) + tensor.shape[1:])


def state_increment(memory, key_block, value_block, running):
    finale = running[-1]
    key_to_end = (key_block.astype(jnp.float32) * jnp.exp(finale[None] - running)).astype(
        jnp.bfloat16
    )
    added = jnp.einsum("shi,shj->hij", key_to_end, value_block, preferred_element_type=jnp.float32)
    return jnp.exp(finale)[:, :, None] * memory + added


def block_pass(query_matrix, key_rows, value_rows, decays, initial):
    triangle = jnp.tril(jnp.ones((GROUP, GROUP), jnp.float32))

    def block_advance(memory, blocks):
        query_block, key_block, value_block, decay_block = blocks
        running = jnp.cumsum(decay_block, axis=0)
        query_decayed = (query_block.astype(jnp.float32) * jnp.exp(running)).astype(jnp.bfloat16)
        key_grown = (key_block.astype(jnp.float32) * jnp.exp(-running)).astype(jnp.bfloat16)
        scores = (
            jnp.einsum("thi,shi->hts", query_decayed, key_grown, preferred_element_type=jnp.float32)
            * triangle
        )
        within = jnp.einsum(
            "hts,shj->thj",
            scores.astype(jnp.bfloat16),
            value_block,
            preferred_element_type=jnp.float32,
        )
        carried = jnp.einsum("thi,hij->thj", query_decayed.astype(jnp.float32), memory)
        memory = state_increment(memory, key_block, value_block, running)
        return (memory, within + carried)

    blocks = tuple((to_blocks(tensor) for tensor in (query_matrix, key_rows, value_rows, decays)))
    last_memory, outputs = lax.scan(block_advance, initial, blocks)
    return outputs.reshape((query_matrix.shape[0],) + outputs.shape[2:])


def device_summary(key_rows, value_rows, decays):
    heads_here = key_rows.shape[1]

    def device_advance(memory, blocks):
        key_block, value_block, decay_block = blocks
        running = jnp.cumsum(decay_block, axis=0)
        return (state_increment(memory, key_block, value_block, running), None)

    initial = jnp.zeros((heads_here, HEAD_K, HEAD_V), jnp.float32)
    memory, unused = lax.scan(
        device_advance,
        initial,
        tuple((to_blocks(tensor) for tensor in (key_rows, value_rows, decays))),
    )
    total = jnp.sum(decays, axis=0)
    return (total.reshape(-1), memory.reshape(-1, memory.shape[2]))


def combine_states(earlier, latter):
    return (earlier[0] + latter[0], jnp.exp(latter[0])[:, None] * earlier[1] + latter[1])


def local(features, w_query, w_key, w_value, w_gate, w_out, forget):
    row_count = features.shape[0]
    heads_here = w_query.shape[1] // HEAD_K
    columns = collect(features, "head", 1)
    query_sum, key_sum, value_sum, gating = tuple(
        (
            jnp.dot(columns, weight, preferred_element_type=jnp.float32)
            for weight in (w_query, w_key, w_value, w_gate)
        )
    )
    query_matrix = (query_sum * 0.125).astype(jnp.bfloat16).reshape(row_count, heads_here, HEAD_K)
    key_rows = key_sum.astype(jnp.bfloat16).reshape(row_count, heads_here, HEAD_K)
    value_rows = value_sum.astype(jnp.bfloat16).reshape(row_count, heads_here, HEAD_V)
    decays = forget.astype(jnp.float32).reshape(2, row_count, heads_here, HEAD_K)
    flipped_queries = jnp.flip(query_matrix, 0)
    flipped_keys = jnp.flip(key_rows, 0)
    flipped_values = jnp.flip(value_rows, 0)
    flipped_decays = jnp.flip(decays[1], 0)
    ahead_total, ahead_memory = device_summary(key_rows, value_rows, decays[0])
    behind_total, behind_memory = device_summary(flipped_keys, flipped_values, flipped_decays)
    identity = (jnp.zeros_like(ahead_total), jnp.zeros_like(ahead_memory))
    ahead_inflow = prefix_by_axis((ahead_total, ahead_memory), SEQ, combine_states, identity)[1]
    behind_inflow = carried_in((behind_total, behind_memory), SEQ, combine_states, identity)[1]
    ahead_out = block_pass(
        query_matrix,
        key_rows,
        value_rows,
        decays[0],
        ahead_inflow.reshape(heads_here, HEAD_K, HEAD_V),
    )
    behind_flipped = block_pass(
        flipped_queries,
        flipped_keys,
        flipped_values,
        flipped_decays,
        behind_inflow.reshape(heads_here, HEAD_K, HEAD_V),
    )
    mixture = ahead_out + jnp.flip(behind_flipped, 0)
    scaled = mixture * lax.rsqrt(jnp.mean(mixture * mixture, axis=-1, keepdims=True) + 1e-06)
    normed = (scaled.reshape(row_count, heads_here * HEAD_V) * jax.nn.silu(gating)).astype(
        jnp.bfloat16
    )
    out_width = w_out.shape[1] // lax.axis_size("head")
    own_columns = lax.dynamic_slice_in_dim(w_out, lax.axis_index("head") * out_width, out_width, 1)
    encoded = jnp.dot(
        lax.all_gather(normed, "head", axis=1, tiled=True),
        own_columns,
        preferred_element_type=jnp.float32,
    )
    return encoded.astype(jnp.bfloat16)


def solution(mesh):
    torus = Mesh(
        mesh.devices.reshape(4, 8, 4, mesh.shape["head"]), ("seq_0", "seq_1", "seq_2", "head")
    )
    placed = (
        P(SEQ, "head"),
        P(None, "head"),
        P(None, "head"),
        P(None, "head"),
        P(None, "head"),
        P(),
        P(None, SEQ, "head"),
    )
    return jax.shard_map(
        local, mesh=torus, in_specs=placed, out_specs=P(SEQ, "head"), check_vma=False
    )
```

profile of v0, /device:TPU:1, one launch (start us, length us, event | category | flops | bytes accessed | tf_op | source)
XLA Modules:
  0.0 234.6 jit_solution(15789298678491646530)
XLA Ops:
  2.0 10.3 %all-to-all-start = ((bf16[4,256,256]{1,2,0:T(8,128)(2,1)}), bf16[4,256,256]{1,2,0:T(8,128)(2,1)S(1)}, u32[]{:S(2)}, u32[]{:S(2)}) async-start(bf16[4,256,256]{1,2,0:T(8,128)(2,1)} %broadcast_in_dim.16), calls=%async_computation | async-start | bytes 1048576 | tf_op jit(solution)/shard_map/all_to_all | solution.py:15
  15.0 11.3 %all-to-all-done = bf16[4,256,256]{1,2,0:T(8,128)(2,1)S(1)} async-done(((bf16[4,256,256]{1,2,0:T(8,128)(2,1)}), bf16[4,256,256]{1,2,0:T(8,128)(2,1)S(1)}, u32[]{:S(2)}, u32[]{:S(2)}) %all-to-all-start) | async-done | bytes 524320 | tf_op jit(solution)/shard_map/all_to_all | solution.py:15
  26.3 1.4 convolution_convert_fusion.1
  28.6 1.2 convolution_convert_fusion.2
  31.3 2.8 %rev.21 = bf16[256,2,128]{2,0,1:T(8,128)(2,1)} reverse(bf16[256,2,128]{2,0,1:T(8,128)(2,1)} %copy.69), dimensions={0} | reverse | bytes 262144 | tf_op jit(solution)/shard_map/jit(_flip)/rev | solution.py:168
  36.0 4.5 %while.51 = (s32[]{:T(128)}, f32[2,64,128]{2,1,0:T(8,128)S(1)}, f32[4,64,2,64]{3,2,1,0:T(2,128)S(1)}, bf16[4,64,2,64]{3,2,1,0:T(2,128)(2,1)}, bf16[4,64,2,128]{3,1,2,0:T(8,128)(2,1)S(1)}, /*index=5*/s32[]{:T(128)}, s32[]{:T(128)}) while((s32[]{:T(128)}, f32[2,64,128]{2,1,0:T(8,128)S(1)}, f32[4,64,2,64]{3,2,1,0:T(2,128)S(1)}, ...), condition=%wide.region_9.10_spmd.clone, body=%wide.region_7.9_spmd.clone.sunk | while | flops 2695171 | bytes 364131 | solution.py:139
  40.6 11.2 %all-gather.9 = bf16[4,129,128]{2,1,0:T(8,128)(2,1)S(1)} all-gather(bf16[1,129,128]{2,1,0:T(8,128)(2,1)S(1)} %maximum_bitcast_fusion.3), channel_id=5, replica_groups=mesh['seq_0'=4,'seq_1'=8,'seq_2'=4,'head'=4] {'seq_2'}, dimensions={0}, use_global_device_ids=true | all-gather | bytes 165120 | tf_op jit(solution)/shard_map/all_gather | solution.py:43
  53.1 25.6 %all-gather.10 = bf16[8,129,128]{2,1,0:T(8,128)(2,1)S(1)} all-gather(bf16[1,129,128]{2,1,0:T(8,128)(2,1)S(1)} %maximum_bitcast_fusion.4), channel_id=6, replica_groups=mesh['seq_0'=4,'seq_1'=8,'seq_2'=4,'head'=4] {'seq_1'}, dimensions={0}, use_global_device_ids=true | all-gather | bytes 297216 | tf_op jit(solution)/shard_map/all_gather | solution.py:43
  80.0 1.7 copy.62
  81.8 1.7 copy.61
  83.5 7.6 %while.50 = (s32[]{:T(128)}, f32[2,64,128]{2,1,0:T(8,128)S(1)}, f32[4,64,2,64]{3,2,1,0:T(2,128)S(1)}, bf16[4,64,2,64]{3,2,1,0:T(2,128)(2,1)}, bf16[4,64,2,128]{3,1,2,0:T(8,128)(2,1)}, /*index=5*/s32[]{:T(128)}, s32[]{:T(128)}) while((s32[]{:T(128)}, f32[2,64,128]{2,1,0:T(8,128)S(1)}, f32[4,64,2,64]{3,2,1,0:T(2,128)S(1)}, ...), condition=%wide.region_2.3_spmd.clone, body=%wide.region_0.2_spmd.clone.sunk | while | flops 2695171 | bytes 347743 | solution.py:139
  91.1 11.0 %all-gather.6 = f32[4,129,128]{2,1,0:T(8,128)S(1)} all-gather(f32[1,129,128]{2,1,0:T(8,128)S(1)} %maximum_bitcast_fusion), channel_id=2, replica_groups=mesh['seq_0'=4,'seq_1'=8,'seq_2'=4,'head'=4] {'seq_2'}, dimensions={0}, use_global_device_ids=true | all-gather | bytes 330240 | tf_op jit(solution)/shard_map/all_gather | solution.py:43
  102.8 1.7 slice_convert_fusion.7
  104.7 19.2 %all-gather.7 = f32[8,129,128]{2,1,0:T(8,128)S(1)} all-gather(f32[1,129,128]{2,1,0:T(8,128)S(1)} %maximum_bitcast_fusion.1), channel_id=3, replica_groups=mesh['seq_0'=4,'seq_1'=8,'seq_2'=4,'head'=4] {'seq_1'}, dimensions={0}, use_global_device_ids=true | all-gather | bytes 594432 | tf_op jit(solution)/shard_map/all_gather | solution.py:43
  125.0 10.0 %all-gather.8 = f32[4,129,128]{2,1,0:T(8,128)S(1)} all-gather(f32[1,129,128]{2,1,0:T(8,128)S(1)} %maximum_bitcast_fusion.2), channel_id=4, replica_groups=mesh['seq_0'=4,'seq_1'=8,'seq_2'=4,'head'=4] {'seq_0'}, dimensions={0}, use_global_device_ids=true | all-gather | bytes 330240 | tf_op jit(solution)/shard_map/all_gather | solution.py:43
  135.9 9.3 %all-gather.11 = bf16[4,129,128]{2,1,0:T(8,128)(2,1)S(1)} all-gather(bf16[1,129,128]{2,1,0:T(8,128)(2,1)S(1)} %maximum_bitcast_fusion.5), channel_id=7, replica_groups=mesh['seq_0'=4,'seq_1'=8,'seq_2'=4,'head'=4] {'seq_0'}, dimensions={0}, use_global_device_ids=true | all-gather | bytes 165120 | tf_op jit(solution)/shard_map/all_gather | solution.py:43
  148.7 1.2 fusion.76
  150.9 1.6 add_add_fusion
  153.2 15.1 %while.48 = (s32[]{:T(128)}, f32[2,64,128]{2,1,0:T(8,128)S(1)}, f32[4,64,2,128]{3,1,0,2:T(8,128)}, f32[4,64,2,64]{3,2,1,0:T(2,128)S(1)}, bf16[4,64,2,64]{3,2,1,0...) while((s32[]{:T(128)}, f32[2,64,128]{2,1,0:T(8,128)S(1)}, ...), condition=%wide.region_6.7_spmd.clone, body=%wide.region_4.6_spmd.clone.sunk | while | flops 8011778 | bytes 774749 | solution.py:126
  154.4 1.6 fusion.262
  158.2 1.6 fusion.262
  161.9 1.6 fusion.262
  165.7 1.6 fusion.262
  179.2 1.6 fusion.81
  181.4 15.1 %while.49 = (s32[]{:T(128)}, f32[2,64,128]{2,1,0:T(8,128)S(1)}, f32[4,64,2,128]{3,1,0,2:T(8,128)}, f32[4,64,2,64]{3,2,1,0:T(2,128)S(1)}, bf16[4,64,2,64]{3,2,1,0...) while((s32[]{:T(128)}, f32[2,64,128]{2,1,0:T(8,128)S(1)}, ...), condition=%wide.region_13.14_spmd.clone, body=%wide.region_11.13_spmd.clone.sunk | while | flops 8011778 | bytes 774749 | solution.py:126
  182.6 1.6 fusion.275
  186.3 1.6 fusion.275
  190.1 1.6 fusion.275
  193.9 1.6 fusion.275
  196.5 1.7 rev.23
  198.6 1.4 fusion.78
  200.0 33.7 %all_gather.51 = bf16[256,1024]{1,0:T(8,128)(2,1)S(1)} all-gather(bf16[256,256]{1,0:T(8,128)(2,1)S(1)} %fusion.78), channel_id=1, replica_groups=mesh['seq_0'=4,'seq_1'=8,'seq_2'=4,'head'=4] {'head'}, dimensions={1}, use_global_device_ids=true | all-gather | bytes 655360 | tf_op jit(solution)/shard_map/all_gather | solution.py:197
  (210 shorter events, 61.0 us)
Async XLA Ops:
  0.0 233.7 %copy-start = (bf16[1024,1024]{1,0:T(8,128)(2,1)S(1)}, bf16[1024,1024]{1,0:T(8,128)(2,1)}, u32[]{:S(2)}) copy-start(bf16[1024,1024]{1,0:T(8,128)(2,1)} %param.20) | copy-start | bytes 6291460
  0.0 12.3 %copy-start.5 = (bf16[2,256,128]{2,1,0:T(8,128)(2,1)S(1)}, bf16[2,256,128]{2,1,0:T(8,128)(2,1)}, u32[]{:S(2)}) copy-start(bf16[2,256,128]{2,1,0:T(8,128)(2,1)} %param.21) | copy-start | bytes 393220
  2.0 24.3 %all-to-all-start = ((bf16[4,256,256]{1,2,0:T(8,128)(2,1)}), bf16[4,256,256]{1,2,0:T(8,128)(2,1)S(1)}, u32[]{:S(2)}, u32[]{:S(2)}) async-start(bf16[4,256,256]{1,2,0:T(8,128)(2,1)} %broadcast_in_dim.16), calls=%async_computation | async-start | bytes 1048576 | tf_op jit(solution)/shard_map/all_to_all | solution.py:15
  40.6 50.6 %copy-start.1 = (bf16[4,64,2,128]{3,1,2,0:T(8,128)(2,1)}, bf16[4,64,2,128]{3,1,2,0:T(8,128)(2,1)S(1)}, u32[]{:S(2)}) copy-start(bf16[4,64,2,128]{3,1,2,0:T(8,128)(2,1)S(1)} %get-tuple-element.688) | copy-start | bytes 393220
  78.7 0.7 copy-start.2
  104.5 31.2 %copy-start.3 = (bf16[8,129,128]{2,1,0:T(8,128)(2,1)S(1)}, bf16[8,129,128]{2,1,0:T(8,128)(2,1)}, u32[]{:S(2)}) copy-start(bf16[8,129,128]{2,1,0:T(8,128)(2,1)} %copy-done.2) | copy-start | bytes 792580
  104.5 31.4 %copy-start.6 = (bf16[1,128]{1,0:T(2,128)(2,1)S(1)}, bf16[1,128]{1,0:T(2,128)(2,1)}, u32[]{:S(2)}) copy-start(bf16[1,128]{1,0:T(2,128)(2,1)} %convert_bitcast_fusion) | copy-start | bytes 772
  153.2 18.0 %copy-start.7 = (f32[1,1,128]{2,1,0:T(1,128)S(1)}, f32[1,1,128]{2,1,0:T(1,128)}, u32[]{:S(2)}) copy-start(f32[1,1,128]{2,1,0:T(1,128)} %get-tuple-element.415) | copy-start | bytes 1540
  153.2 24.7 %copy-start.10 = (f32[128]{0:T(128)S(1)}, f32[128]{0:T(128)}, u32[]{:S(2)}) copy-start(f32[128]{0:T(128)} %get-tuple-element.307) | copy-start | bytes 1540
  153.2 24.8 %copy-start.9 = (f32[128]{0:T(128)S(1)}, f32[128]{0:T(128)}, u32[]{:S(2)}) copy-start(f32[128]{0:T(128)} %get-tuple-element.308) | copy-start | bytes 1540
  153.2 24.8 %copy-start.8 = (f32[128]{0:T(128)S(1)}, f32[128]{0:T(128)}, u32[]{:S(2)}) copy-start(f32[128]{0:T(128)} %get-tuple-element.306) | copy-start | bytes 1540
  181.4 16.8 %copy-start.4 = (f32[4,64,2,128]{3,1,0,2:T(8,128)S(1)}, f32[4,64,2,128]{3,1,0,2:T(8,128)}, u32[]{:S(2)}) copy-start(f32[4,64,2,128]{3,1,0,2:T(8,128)} %get-tuple-element.144) | copy-start | bytes 786436
where the time goes:
time: 238 us; the launch traced here: 235 us
  blocking collectives  120 us (50%)
  matrix products  32.7 us (14%)
  local copies, waits for them, and re-layouts  32.1 us (13%)
  other arithmetic  27.5 us (12%)
  waiting for transfers between devices  11.3 us (5%)
  starting transfers between devices  10.3 us (4%)
    all_gather x6, blocking collectives, gathered_once(): both, at, found = (lax.all_gather(jnp.concatenate(lines), axis), 0, {})  86.3 us
    all_gather x1, blocking collectives, local(): lax.all_gather(normed, 'head', axis=1, tiled=True)  33.7 us
    dot_general x8, matrix products, block_advance(): jnp.einsum('hts,shj->thj', scores.astype(jnp.bfloat16), value_block, pref...  13.2 us
    dot_general x16, matrix products, state_increment(): jnp.einsum('shi,shj->hij', key_to_end, value_block, preferred_element_typ...  12.3 us
    all_to_all x1, waiting for transfers between devices, from_everyone(): return lax.all_to_all(copies, axis, split_axis=0, concat_axis=0, tiled=True)  11.3 us
    all_to_all x1, starting transfers between devices, from_everyone(): return lax.all_to_all(copies, axis, split_axis=0, concat_axis=0, tiled=True)  10.3 us
    exp x31, local copies, waits for them, and re-layouts, combine_states(): jnp.exp(latter[0])[:, None] * earlier[1] + latter[1]  9.35 us
    convert_element_type x8, other arithmetic, block_advance(): (key_block.astype(jnp.float32) * jnp.exp(-running)).astype(jnp.bfloat16)  7.31 us
  transfers between devices with their start and end apart: 1, of which 1 were waited for; matrix products, arithmetic and copies ran while one was open for 1% of the time, Pallas kernels for 0%

commit v1 on v0

v1 whole, which is shorter than its diff:
```python
import functools

import jax
import jax.numpy as jnp
from jax import lax
from jax.experimental import pallas as pl
from jax.experimental.pallas import tpu as pltpu
from jax.sharding import Mesh
from jax.sharding import PartitionSpec as P

HEAD_K = 64
HEAD_V = 128
GROUP = 64
SEQ = ("x", "z", "yl")
HEAD = ("yh", "c")
MESH = pl.DeviceIdType.MESH
F32 = jnp.float32
BF16 = jnp.bfloat16
CHUNKS = 4


def dot(a, b, dims):
    return lax.dot_general(a, b, (dims, ((), ())), preferred_element_type=F32)


def mm(a, b):
    return dot(a, b, ((1,), (0,)))


def mm_t(a, b):
    return dot(a, b, ((1,), (1,)))


def t_mm(a, b):
    return dot(a, b, ((0,), (0,)))


def kernel(
    sizes,
    feats, wq, wk, wv, wg, wout, fg,
    out,
    fa, na, w, wo, fgv, acc, ex, kb, qb, vb, sg, base,
    y1s, y1r, ypre, zs, zr, xs, xr, y2s, y2r,
    load_sem, d_send, d_recv, r_send, r_recv, f_send, f_recv,
    y1_send, y1_recv, z_send, z_recv, x_send, x_recv, y2_send, y2_recv,
):
    nx, nz, ny = sizes
    tok, dcol = feats.shape
    kw = wq.shape[1]
    vw = wv.shape[1]
    pr = HEAD_V // ny
    rows = tok // CHUNKS
    blocks = tok // GROUP
    x, z, yl = lax.axis_index("x"), lax.axis_index("z"), lax.axis_index("yl")
    yh, c = lax.axis_index("yh"), lax.axis_index("c")
    h = yh * 2 + c
    h1 = yh * 2 + (1 - c)
    h2 = (1 - yh) * 2 + c
    h3 = (1 - yh) * 2 + (1 - c)

    def load(k, src, dst):
        return pltpu.make_async_copy(src, dst, load_sem.at[k])

    loads = [
        load(0, feats, fa.at[h]),
        load(1, fg, fgv),
        load(2, wk, w.at[:, pl.ds(0, kw)]),
        load(3, wv, w.at[:, pl.ds(kw, vw)]),
        load(4, wq, w.at[:, pl.ds(kw + vw, kw)]),
        load(5, wg, w.at[:, pl.ds(2 * kw + vw, vw)]),
        load(6, wout.at[:, pl.ds(pl.multiple_of(h * dcol, dcol), dcol)], wo),
    ]
    for item in loads:
        item.start()

    barrier = pltpu.get_barrier_semaphore()
    partners = [{"c": 1 - c}, {"yh": 1 - yh}]
    partners += [{"yl": lax.rem(yl + d, ny)} for d in range(1, ny)]
    partners += [{"z": lax.rem(z + d, nz)} for d in range(1, nz)]
    partners += [{"x": lax.rem(x + d, nx)} for d in range(1, nx)]
    for partner in partners:
        pl.semaphore_signal(barrier, inc=1, device_id=partner, device_id_type=MESH)
    pl.semaphore_wait(barrier, len(partners))

    def remote(src, dst, ss, rs, where):
        return pltpu.make_async_remote_copy(
            src_ref=src, dst_ref=dst, send_sem=ss, recv_sem=rs,
            device_id=where, device_id_type=MESH,
        )

    def part(buf, slot, n):
        return buf.at[slot, pl.ds(n * rows, rows)]

    core, across = {"c": 1 - c}, {"yh": 1 - yh}

    def direct(e, buf, n):
        piece = part(buf, h, n)
        return remote(piece, piece, d_send.at[e, n], d_recv.at[e, n], core)

    def far(e, buf, slot, n):
        piece = part(buf, slot, n)
        return remote(piece, piece, r_send.at[e, n], r_recv.at[e, n], across)

    def passed(e, buf, slot, n):
        piece = part(buf, slot, n)
        return remote(piece, piece, f_send.at[e, n], f_recv.at[e, n], core)

    def arrived_direct(e, buf, n):
        piece = part(buf, h1, n)
        remote(piece, piece, d_send.at[e, n], d_recv.at[e, n], core).wait_recv()

    loads[0].wait()
    for n in range(CHUNKS):
        far(0, fa, h, n).start()
    for n in range(CHUNKS):
        direct(0, fa, n).start()

    loads[1].wait()
    ti = lax.broadcasted_iota(jnp.int32, (tok, tok), 0)
    tj = lax.broadcasted_iota(jnp.int32, (tok, tok), 1)
    same = (ti // GROUP) == (tj // GROUP)

    def sums(mask, which):
        return mm(jnp.where(mask, 1.0, 0.0).astype(BF16), fgv[which])

    full = sums(tj <= ti, 0)
    total_f = full[tok - 1 : tok]
    ex[0] = jnp.exp(full)
    ex[1] = jnp.exp(sums(tj > ti, 0))
    inside = sums(same & (tj <= ti), 0)
    ex[2] = jnp.exp(inside)
    ex[3] = jnp.exp(-inside)
    ex[4] = jnp.exp(sums(same & (tj > ti), 0))
    full = sums(tj >= ti, 1)
    total_r = full[0:1]
    ex[5] = jnp.exp(full)
    ex[6] = jnp.exp(sums(tj < ti, 1))
    inside = sums(same & (tj >= ti), 1)
    ex[7] = jnp.exp(inside)
    ex[8] = jnp.exp(-inside)
    ex[9] = jnp.exp(sums(same & (tj < ti), 1))

    def packed(lf, lr):
        row = lax.broadcasted_iota(jnp.int32, (8, kw), 0)
        hf, hr = lf.astype(BF16).astype(F32), lr.astype(BF16).astype(F32)
        block = jnp.where(row == 0, hf, 0.0)
        block = jnp.where(row == 1, lf - hf, block)
        block = jnp.where(row == 2, hr, block)
        return jnp.where(row == 3, lr - hr, block).astype(BF16)

    def unpacked(ref, at):
        rows8 = ref[at, pl.ds(2 * pr, 8)].astype(F32)
        return rows8[0:1] + rows8[1:2], rows8[2:3] + rows8[3:4]

    for k in range(2, 6):
        loads[k].wait()

    def weights(slot):
        return pl.ds(pl.multiple_of(slot * dcol, dcol), dcol)

    acc[...] = mm(fa[h], w[weights(h)])
    for n in range(CHUNKS):
        arrived_direct(0, fa, n)
    acc[...] += mm(fa[h1], w[weights(h1)])

    kv = kw + vw
    for n in range(CHUNKS):
        far(0, fa, h2, n).wait_recv()
        passed(0, fa, h2, n).start()
        passed(0, fa, h3, n).wait_recv()
        span = pl.ds(n * rows, rows)
        got = (
            acc[span, pl.ds(0, kv)]
            + mm(fa[h2, span], w[weights(h2), pl.ds(0, kv)])
            + mm(fa[h3, span], w[weights(h3), pl.ds(0, kv)])
        )
        kb[span] = got[:, 0:kw].astype(BF16)
        vb[span] = got[:, kw:kv].astype(BF16)

    lane = lax.broadcasted_iota(jnp.int32, (HEAD_V, kw), 1)
    first = lane < HEAD_K

    def own_heads(both):
        top, low = both[0:HEAD_V], both[HEAD_V : 2 * HEAD_V]
        return (
            jnp.where(first, top[:, 0:kw], low[:, 0:kw]),
            jnp.where(first, top[:, kw : 2 * kw], low[:, kw : 2 * kw]),
        )

    keys = kb[...].astype(F32)
    ended = jnp.concatenate(
        [(keys * ex[1]).astype(BF16), (keys * ex[6]).astype(BF16)], axis=1
    )
    mem_f, mem_r = own_heads(t_mm(vb[...], ended))
    decay_rows = packed(total_f, total_r)
    for j in range(ny):
        y1s[j, pl.ds(0, pr)] = mem_f[j * pr : (j + 1) * pr].astype(BF16)
        y1s[j, pl.ds(pr, pr)] = mem_r[j * pr : (j + 1) * pr].astype(BF16)
        y1s[j, pl.ds(2 * pr, 8)] = decay_rows

    def to_all(n, me, axis, send, slot_of, recv, ss, rs):
        for d in range(1, n):
            to = lax.rem(me + d, n)
            remote(send.at[slot_of(to)], recv.at[me], ss.at[d], rs.at[me], {axis: to}).start()

    def from_all(n, me, axis, recv, ss, rs):
        for d in range(1, n):
            src = lax.rem(me + n - d, n)
            remote(recv.at[src], recv.at[src], ss.at[d], rs.at[src], {axis: src}).wait_recv()

    def sent_all(n, me, axis, send, slot_of, recv, ss, rs):
        for d in range(1, n):
            to = lax.rem(me + d, n)
            remote(send.at[slot_of(to)], recv.at[me], ss.at[d], rs.at[me], {axis: to}).wait_send()

    to_all(ny, yl, "yl", y1s, lambda to: to, y1r, y1_send, y1_recv)
    y1r[yl] = y1s[yl]

    qg = (
        acc[:, pl.ds(kv, kv)]
        + mm(fa[h2], w[weights(h2), pl.ds(kv, kv)])
        + mm(fa[h3], w[weights(h3), pl.ds(kv, kv)])
    )
    qb[...] = (qg[:, 0:kw] * 0.125).astype(BF16)
    gate = qg[:, kw:kv]
    sg[...] = gate / (1.0 + jnp.exp(-gate))

    from_all(ny, yl, "yl", y1r, y1_send, y1_recv)

    def walk(ref, order, which):
        state = jnp.zeros((pr, kw), F32)
        log = jnp.zeros((1, kw), F32)
        before = {}
        for j in order:
            before[j] = (state, log)
            step = unpacked(ref, j)[which]
            state = state * jnp.exp(step) + ref[j, pl.ds(which * pr, pr)].astype(F32)
            log = log + step
        return before, state, log

    before_f, state_f, log_f = walk(y1r, range(ny), 0)
    before_r, state_r, log_r = walk(y1r, range(ny)[::-1], 1)
    zs[pl.ds(0, pr)] = state_f.astype(BF16)
    zs[pl.ds(pr, pr)] = state_r.astype(BF16)
    zs[pl.ds(2 * pr, 8)] = packed(log_f, log_r)
    for d in range(1, nz):
        to = lax.rem(z + d, nz)
        remote(zs, zr.at[z], z_send.at[d], z_recv.at[z], {"z": to}).start()
    zr[z] = zs[...]

    queries = qb[...].astype(F32)
    keys = kb[...].astype(F32)
    qd = jnp.concatenate(
        [(queries * ex[2]).astype(BF16), (queries * ex[7]).astype(BF16)], axis=1
    )
    kd_f = (keys * ex[3]).astype(BF16)
    kd_r = (keys * ex[8]).astype(BF16)
    wide = lax.broadcasted_iota(jnp.int32, (tok, kw), 1) < HEAD_K
    ke = jnp.concatenate(
        [(keys * ex[4]).astype(BF16), (keys * ex[9]).astype(BF16)], axis=1
    )
    zero_b = jnp.zeros((), BF16)
    for head in range(2):
        mine = wide if head == 0 else jnp.logical_not(wide)
        s_f = mm_t(jnp.where(mine, qd[:, 0:kw], zero_b), kd_f)
        s_r = mm_t(jnp.where(mine, qd[:, kw : 2 * kw], zero_b), kd_r)
        scores = jnp.where(same & (tj <= ti), s_f, 0.0) + jnp.where(same & (tj >= ti), s_r, 0.0)
        span = pl.ds(head * HEAD_V, HEAD_V)
        base[:, span] = mm(scores.astype(BF16), vb[:, span])

    added = []
    for b in range(blocks):
        at = slice(b * GROUP, (b + 1) * GROUP)
        added.append(own_heads(t_mm(vb[at], ke[at])))
    held_f, held_r = {}, {}
    state = jnp.zeros((HEAD_V, kw), F32)
    for b in range(blocks):
        held_f[b] = state
        last = b * GROUP + GROUP - 1
        state = state * ex[2, last : last + 1] + added[b][0]
    state = jnp.zeros((HEAD_V, kw), F32)
    for b in range(blocks)[::-1]:
        held_r[b] = state
        last = b * GROUP
        state = state * ex[7, last : last + 1] + added[b][1]
    halves = lax.rem(lax.broadcasted_iota(jnp.int32, (HEAD_V, 2 * kw), 1), kw) < HEAD_K

    def split_heads(both):
        return jnp.concatenate(
            [jnp.where(halves, both, zero_b), jnp.where(halves, zero_b, both)], axis=0
        )

    for b in range(blocks):
        at = slice(b * GROUP, (b + 1) * GROUP)
        both = jnp.concatenate([held_f[b].astype(BF16), held_r[b].astype(BF16)], axis=1)
        base[at] += mm_t(qd[at], split_heads(both))

    for d in range(1, nz):
        src = lax.rem(z + nz - d, nz)
        remote(zr.at[src], zr.at[src], z_send.at[d], z_recv.at[src], {"z": src}).wait_recv()

    def reach(ref, n, me, which):
        state = ahead = jnp.zeros((pr, kw), F32)
        log = ahead_log = jnp.zeros((1, kw), F32)
        for k in range(n) if which == 0 else range(n)[::-1]:
            ahead = jnp.where(k == me, state, ahead)
            ahead_log = jnp.where(k == me, log, ahead_log)
            step = unpacked(ref, k)[which]
            state = state * jnp.exp(step) + ref[k, pl.ds(which * pr, pr)].astype(F32)
            log = log + step
        return ahead, ahead_log, state, log

    zf, zlog_f, state_f, log_f = reach(zr, nz, z, 0)
    zb, zlog_r, state_r, log_r = reach(zr, nz, z, 1)
    xs[pl.ds(0, pr)] = state_f.astype(BF16)
    xs[pl.ds(pr, pr)] = state_r.astype(BF16)
    xs[pl.ds(2 * pr, 8)] = packed(log_f, log_r)
    for d in range(1, nx):
        to = lax.rem(x + d, nx)
        remote(xs, xr.at[x], x_send.at[d], x_recv.at[x], {"x": to}).start()
    xr[x] = xs[...]
    for d in range(1, nx):
        src = lax.rem(x + nx - d, nx)
        remote(xr.at[src], xr.at[src], x_send.at[d], x_recv.at[src], {"x": src}).wait_recv()
    xf = reach(xr, nx, x, 0)[0]
    xb = reach(xr, nx, x, 1)[0]
    come_f = xf * jnp.exp(zlog_f) + zf
    come_r = xb * jnp.exp(zlog_r) + zb
    for j in range(ny):
        state, log = before_f[j]
        y2s[j, pl.ds(0, pr)] = (come_f * jnp.exp(log) + state).astype(BF16)
        state, log = before_r[j]
        y2s[j, pl.ds(pr, pr)] = (come_r * jnp.exp(log) + state).astype(BF16)
    to_all(ny, yl, "yl", y2s, lambda to: to, y2r, y2_send, y2_recv)
    y2r[yl] = y2s[yl]
    queries = qb[...].astype(F32)
    qx = jnp.concatenate(
        [(queries * ex[0]).astype(BF16), (queries * ex[5]).astype(BF16)], axis=1
    )
    from_all(ny, yl, "yl", y2r, y2_send, y2_recv)
    inflow = jnp.concatenate(
        [
            jnp.concatenate([y2r[j, pl.ds(0, pr)], y2r[j, pl.ds(pr, pr)]], axis=1)
            for j in range(ny)
        ],
        axis=0,
    )
    inflow = split_heads(inflow)

    for n in range(CHUNKS):
        at = slice(n * rows, (n + 1) * rows)
        mixed = base[at] + mm_t(qx[at], inflow)
        for head in range(2):
            span = slice(head * HEAD_V, (head + 1) * HEAD_V)
            mine = mixed[:, span]
            level = jnp.mean(mine * mine, axis=-1, keepdims=True)
            scaled = mine * lax.rsqrt(level + 1e-06)
            na[h, at, span] = (scaled * sg[at, span]).astype(BF16)
        far(1, na, h, n).start()
        direct(1, na, n).start()

    loads[6].wait()
    acc[:, pl.ds(0, dcol)] = mm(na[h], wo[weights(h)])
    for n in range(CHUNKS):
        arrived_direct(1, na, n)
    acc[:, pl.ds(0, dcol)] += mm(na[h1], wo[weights(h1)])
    for n in range(CHUNKS):
        far(1, na, h2, n).wait_recv()
        passed(1, na, h2, n).start()
        passed(1, na, h3, n).wait_recv()
        at = pl.ds(n * rows, rows)
        out[at] = (
            acc[at, pl.ds(0, dcol)]
            + mm(na[h2, at], wo[weights(h2)])
            + mm(na[h3, at], wo[weights(h3)])
        ).astype(BF16)

    for e, buf in ((0, fa), (1, na)):
        for n in range(CHUNKS):
            direct(e, buf, n).wait_send()
            far(e, buf, h, n).wait_send()
            passed(e, buf, h2, n).wait_send()
    sent_all(ny, yl, "yl", y1s, lambda to: to, y1r, y1_send, y1_recv)
    sent_all(ny, yl, "yl", y2s, lambda to: to, y2r, y2_send, y2_recv)
    for d in range(1, nz):
        to = lax.rem(z + d, nz)
        remote(zs, zr.at[z], z_send.at[d], z_recv.at[z], {"z": to}).wait_send()
    for d in range(1, nx):
        to = lax.rem(x + d, nx)
        remote(xs, xr.at[x], x_send.at[d], x_recv.at[x], {"x": to}).wait_send()


def local(sizes, features, w_query, w_key, w_value, w_gate, w_out, forget):
    nx, nz, ny = sizes
    tok, dcol = features.shape
    depth, kw = w_query.shape
    vw = w_value.shape[1]
    pr = HEAD_V // ny
    msg = 2 * pr + 8
    dma = pltpu.SemaphoreType.DMA
    return pl.pallas_call(
        functools.partial(kernel, sizes),
        out_shape=jax.ShapeDtypeStruct((tok, dcol), BF16),
        in_specs=[pl.BlockSpec(memory_space=pl.ANY)] * 7,
        out_specs=pl.BlockSpec(memory_space=pltpu.VMEM),
        scratch_shapes=[
            pltpu.VMEM((4, tok, dcol), BF16),
            pltpu.VMEM((4, tok, vw), BF16),
            pltpu.VMEM((depth, 2 * (kw + vw)), BF16),
            pltpu.VMEM((4 * vw, dcol), BF16),
            pltpu.VMEM((2, tok, kw), BF16),
            pltpu.VMEM((tok, 2 * (kw + vw)), F32),
            pltpu.VMEM((10, tok, kw), F32),
            pltpu.VMEM((tok, kw), BF16),
            pltpu.VMEM((tok, kw), BF16),
            pltpu.VMEM((tok, vw), BF16),
            pltpu.VMEM((tok, vw), F32),
            pltpu.VMEM((tok, vw), F32),
            pltpu.VMEM((ny, msg, kw), BF16),
            pltpu.VMEM((ny, msg, kw), BF16),
            pltpu.VMEM((8, kw), F32),
            pltpu.VMEM((msg, kw), BF16),
            pltpu.VMEM((nz, msg, kw), BF16),
            pltpu.VMEM((msg, kw), BF16),
            pltpu.VMEM((nx, msg, kw), BF16),
            pltpu.VMEM((ny, 2 * pr, kw), BF16),
            pltpu.VMEM((ny, 2 * pr, kw), BF16),
            dma((7,)),
            dma((2, CHUNKS)), dma((2, CHUNKS)),
            dma((2, CHUNKS)), dma((2, CHUNKS)),
            dma((2, CHUNKS)), dma((2, CHUNKS)),
            dma((ny,)), dma((ny,)),
            dma((nz,)), dma((nz,)),
            dma((nx,)), dma((nx,)),
            dma((ny,)), dma((ny,)),
        ],
        compiler_params=pltpu.CompilerParams(
            collective_id=0, has_side_effects=True, vmem_limit_bytes=60 * 1024 * 1024
        ),
        name="layer",
    )(features, w_query, w_key, w_value, w_gate, w_out, forget)


def solution(mesh, sizes=(4, 8, 4)):
    torus = Mesh(mesh.devices.reshape(*sizes, 2, 2), ("x", "z", "yl", "yh", "c"))
    placed = (
        P(SEQ, HEAD),
        P(None, HEAD),
        P(None, HEAD),
        P(None, HEAD),
        P(None, HEAD),
        P(),
        P(None, SEQ, HEAD),
    )
    return jax.shard_map(
        functools.partial(local, sizes),
        mesh=torus, in_specs=placed, out_specs=P(SEQ, HEAD), check_vma=False,
    )
```

time: 238 us -> 58 us (0.24); the launches traced: 235 us -> 57.9 us
  blocking collectives: 120 us -> 0 us
  Pallas kernels: 0 us -> 56.3 us
  matrix products: 32.7 us -> 0 us
  local copies, waits for them, and re-layouts: 32.1 us -> 1.57 us
  other arithmetic: 27.5 us -> 0 us
  waiting for transfers between devices: 11.3 us -> 0 us
  starting transfers between devices: 10.3 us -> 0 us
    all_gather x7 -> x0, blocking collectives: 120 us -> none  [the longest x6 86.3 us: gathered_once(): both, at, found = (lax.all_gather(jnp.concatenate(lines), axis), 0, {})]
    pallas_call x0 -> x1, Pallas kernels: none -> 56.3 us  [local(): pl.pallas_call(functools.partial(kernel, sizes), out_shape=jax.ShapeDtype...]
    dot_general x37 -> x0, matrix products: 32.7 us -> none  [the longest x8 13.2 us: block_advance(): jnp.einsum('hts,shj->thj', scores.astype(jnp.bfloat16), value_block, pref...]
    convert_element_type x23 -> x0, other arithmetic: 18 us -> none  [the longest x8 7.31 us: block_advance(): (key_block.astype(jnp.float32) * jnp.exp(-running)).astype(jnp.bfloat16)]
    all_to_all x1 -> x0, waiting for transfers between devices: 11.3 us -> none  [from_everyone(): return lax.all_to_all(copies, axis, split_axis=0, concat_axis=0, tiled=True)]
    all_to_all x1 -> x0, starting transfers between devices: 10.3 us -> none  [from_everyone(): return lax.all_to_all(copies, axis, split_axis=0, concat_axis=0, tiled=True)]
    exp x47 -> x0, local copies, waits for them, and re-layouts: 9.42 us -> none  [the longest x31 9.35 us: combine_states(): jnp.exp(latter[0])[:, None] * earlier[1] + latter[1]]
    rev x7 -> x0, local copies, waits for them, and re-layouts: 6.69 us -> none  [the longest x1 2.75 us: local(): flipped_values = jnp.flip(value_rows, 0)]
  transfers between devices with their start and end apart: 1 -> 0, of which waited for: 1 -> 0; matrix products, arithmetic and copies ran while one was open for 1% -> 0% of each run, Pallas kernels for 0% -> 0%
where the time goes in v1:
time: 58 us; the launch traced here: 57.9 us
  Pallas kernels  56.3 us (97%)
  local copies, waits for them, and re-layouts  1.57 us (3%)
    pallas_call x1, Pallas kernels, local(): pl.pallas_call(functools.partial(kernel, sizes), out_shape=jax.ShapeDtype...  56.3 us
    unnamed x1, local copies, waits for them, and re-layouts  1.57 us

profile of v1, /device:TPU:1, one launch (start us, length us, event | category | flops | bytes accessed | tf_op | source)
XLA Modules:
  0.0 57.9 jit_solution(14006989982131131903)
XLA Ops:
  0.0 56.3 %layer.1 = bf16[256,256]{1,0:T(8,128)(2,1)} custom-call(bf16[256,256]{1,0:T(8,128)(2,1)} %feats.1, bf16[1024,128]{1,0:T(8,128)(2,1)} %wq.1, bf16[1024,128]{1,0:T(8,128)(2,1)} %wk.1, bf16[1024,256]{1,0:T(8,128)(2,1)} %wv.1, bf16[1024,256]{1,0:T(8,128)(2,1)} %wg.1, bf16[1024,1024]{1,0:T(8,128)(2,1)} %wout.1, bf16[2,256,128]{2,1,0:T(8,128)(2,1)} %fg.1), custom_call_target="tpu_custom_call" | custom-call | tf_op jit(solution)/shard_map/layer/pallas_call | solution.py:401
  56.3 1.6 %copy.9 = bf16[256,256]{1,0:T(8,128)(2,1)} copy(bf16[256,256]{1,0:T(8,128)(2,1)} %layer.1) | data formatting | bytes 262144
